TPU v7x, 32 devices: a whole 2x2x4 slice. The times are simulated.
32 devices in a mesh: dp: 16 (over z, x, core), mp: 2 (over y).
Axes of the slice: x: 2, y: 2, z: 4, core: 2. Of those that a mesh axis runs over, the one named last changes fastest.
Arguments:
- queries: bfloat16 [12288, 1024], P('dp', 'mp'), may hold values from -3 to 3
- passages: bfloat16 [12288, 1024], P('dp', 'mp'), may hold values from -3 to 3
- positive: int32 [12288], P('dp'), may hold values from 0 to 12287
Outputs:
- grad_queries: bfloat16 [12288, 1024], P('dp', 'mp')
- grad_passages: bfloat16 [12288, 1024], P('dp', 'mp')
All inputs are finite; a program needn't handle non-finite values.
Results may differ from a plain program's by a relative error of at most 0.0034.
Values may be sent and summed in bfloat16 or wider, within the bound.
A program may use at most 128 MiB of HBM per device.

v0:
```python
import math

import jax
import jax.numpy as jnp
from jax import lax
from jax.sharding import PartitionSpec as P


def local(queries, passages, positive):
    group_rows, slice_width = queries.shape
    group_count = lax.axis_size("dp")
    model_index = lax.axis_index("mp")
    relaid = lax.all_to_all(passages, "mp", split_axis=0, concat_axis=1, tiled=True)
    short_rows = relaid.shape[0]
    wide_queries = lax.all_gather(queries, "mp", axis=1, tiled=True)
    passage_block = lax.all_gather(relaid, "dp", axis=0, tiled=True)
    full_width = wide_queries.shape[1]
    logit_scale = 3.0 / math.sqrt(full_width)
    scores = (
        lax.dot_general(
            wide_queries,
            passage_block,
            (((1,), (1,)), ((), ())),
            preferred_element_type=jnp.float32,
        )
        * logit_scale
    )
    local_max = jnp.max(scores, axis=1)
    highest = lax.pmax(local_max, "mp")
    row_total = lax.psum(jnp.sum(jnp.exp(scores - highest[:, None]), axis=1), "mp")
    log_total = highest + jnp.log(row_total)
    column_pos = jnp.arange(group_count * short_rows, dtype=jnp.int32)
    column_ids = (
        column_pos // short_rows * group_rows + model_index * short_rows + column_pos % short_rows
    )
    onehot = (column_ids[None, :] == positive[:, None]).astype(jnp.float32)
    softmax_grad = (jnp.exp(scores - log_total[:, None]) - onehot).astype(jnp.bfloat16)
    query_terms = jnp.dot(softmax_grad, passage_block, preferred_element_type=jnp.float32)
    grad_queries = lax.psum_scatter(query_terms, "mp", scatter_dimension=1, tiled=True).astype(
        jnp.bfloat16
    )
    group_index = lax.axis_index("dp")
    own_passages = lax.all_gather(passages, "mp", axis=1, tiled=True)
    query_relaid = lax.all_to_all(queries, "mp", split_axis=0, concat_axis=1, tiled=True)
    all_queries = lax.all_gather(query_relaid, "dp", axis=0, tiled=True)
    own_log = lax.dynamic_slice_in_dim(log_total, model_index * short_rows, short_rows)
    own_targets = lax.dynamic_slice_in_dim(positive, model_index * short_rows, short_rows).astype(
        jnp.float32
    )
    all_log, all_targets = (
        lax.all_gather(own_log, "dp", axis=0, tiled=True),
        lax.all_gather(own_targets, "dp", axis=0, tiled=True),
    )
    own_scores = (
        lax.dot_general(
            all_queries, own_passages, (((1,), (1,)), ((), ())), preferred_element_type=jnp.float32
        )
        * logit_scale
    )
    own_ids = (group_index * group_rows + jnp.arange(group_rows, dtype=jnp.int32)).astype(
        jnp.float32
    )
    own_hits = (own_ids[None, :] == all_targets[:, None]).astype(jnp.float32)
    own_grad = (jnp.exp(own_scores - all_log[:, None]) - own_hits).astype(jnp.bfloat16)
    own_terms = lax.dot_general(
        own_grad, all_queries, (((0,), (0,)), ((), ())), preferred_element_type=jnp.float32
    )
    grad_passages = lax.psum_scatter(own_terms, "mp", scatter_dimension=1, tiled=True).astype(
        jnp.bfloat16
    )
    return (grad_queries, grad_passages)


def solution(mesh):
    return jax.shard_map(
        local,
        mesh=mesh,
        in_specs=(P("dp", "mp"), P("dp", "mp"), P("dp")),
        out_specs=(P("dp", "mp"), P("dp", "mp")),
        check_vma=False,
    )
```

profile of v0, /device:TPU:0, one launch (start us, length us, event | category | flops | bytes accessed | tf_op | source)
XLA Modules:
  0.0 386.7 jit_solution(6232111345295241433)
XLA Ops:
  7.2 0.7 all-gather.7.cloned.1.call-update
  7.9 18.1 %all_to_all.38 = bf16[2,384,512]{2,1,0:T(8,128)(2,1)S(1)} all-to-all(bf16[2,384,512]{2,1,0:T(8,128)(2,1)} %bitcast.24), channel_id=1, replica_groups=mesh['dp'=16,'mp'=2] {'mp'}, dimensions={0} | all-to-all | bytes 1572864 | tf_op jit(solution)/shard_map/all_to_all | solution.py:13
  26.0 1.2 copy.7
  27.3 0.7 all-gather.13.cloned.1.call-update
  28.0 21.1 %all_to_all.39 = bf16[2,384,512]{2,1,0:T(8,128)(2,1)S(1)} all-to-all(bf16[2,384,512]{2,1,0:T(8,128)(2,1)} %bitcast.23), channel_id=1, replica_groups=mesh['dp'=16,'mp'=2] {'mp'}, dimensions={0} | all-to-all | bytes 1572864 | tf_op jit(solution)/shard_map/all_to_all | solution.py:44
  49.1 1.2 copy.8
  50.3 0.0 reduce-scatter.3.cloned.1.call-start
  50.3 0.8 dynamic-slice_convert_fusion
  51.1 22.4 %all-gather.1 = f32[16,1,384]{2,1,0:T(1,128)S(1)} all-gather(f32[1,1,384]{2,1,0:T(1,128)S(1)} %reshape.42), channel_id=1, replica_groups=mesh['dp'=16,'mp'=2] {'dp'}, dimensions={0}, use_global_device_ids=true | all-gather | bytes 26112 | tf_op jit(solution)/shard_map/all_gather | solution.py:52
  73.5 81.4 %all-gather.9.cloned.1.call-done = bf16[6144,1024]{0,1:T(8,128)(2,1)} async-done(((bf16[384,1024]{0,1:T(8,128)(2,1)}), bf16[6144,1024]{0,1:T(8,128)(2,1)}) %all-gather.9.cloned.1.call-update) | async-done | bytes 12582928 | tf_op jit(solution)/shard_map/all_gather | solution.py:16
  154.9 16.9 %multiply_reduce_fusion = (f32[768]{0:T(1024)S(1)}, f32[768,6144]{1,0:T(8,128)}) fusion(bf16[768,1024]{1,0:T(8,128)(2,1)} %all-gather.7.cloned.1.call-done, bf16[6144,1024]{0,1:T(8,128)(2,1)} %all-gather.9.cloned.1.call-done), kind=kOutput, calls=%fused_computation.3 | convolution fusion | flops 9673112576 | bytes 33033216 | tf_op jit(solution)/shard_map/dot_general | solution.py:20
  171.9 5.2 %pmax.7 = f32[768]{0:T(1024)S(1)} all-reduce(f32[768]{0:T(1024)S(1)} %get-tuple-element.2), channel_id=1, replica_groups=mesh['dp'=16,'mp'=2] {'mp'}, use_global_device_ids=true, to_apply=%region_1.0 | all-reduce | flops 768 | bytes 6144 | tf_op jit(solution)/shard_map/pmax | solution.py:29
  177.1 9.5 %exponential_reduce_fusion = f32[768]{0:T(1024)S(1)} fusion(f32[768,6144]{1,0:T(8,128)} %get-tuple-element.3, f32[768]{0:T(1024)S(1)} %pmax.7), kind=kLoop, calls=%fused_computation.2 | loop fusion | flops 14155008 | bytes 18880512 | tf_op jit(solution)/shard_map/reduce_sum | solution.py:30
  186.7 4.9 %psum.7 = f32[768]{0:T(1024)S(1)} all-reduce(f32[768]{0:T(1024)S(1)} %exponential_reduce_fusion), channel_id=1, replica_groups=mesh['dp'=16,'mp'=2] {'mp'}, use_global_device_ids=true, to_apply=%region_3.0 | all-reduce | flops 768 | bytes 6144 | tf_op jit(solution)/shard_map/psum | solution.py:30
  191.6 0.1 dynamic_slice.6
  191.7 19.4 %all-gather = f32[16,1,384]{2,1,0:T(1,128)S(1)} all-gather(f32[1,1,384]{2,1,0:T(1,128)S(1)} %reshape.40), channel_id=1, replica_groups=mesh['dp'=16,'mp'=2] {'dp'}, dimensions={0}, use_global_device_ids=true | all-gather | bytes 26112 | tf_op jit(solution)/shard_map/all_gather | solution.py:51
  211.1 18.8 %fusion = f32[768,1024]{1,0:T(8,128)} fusion(bf16[6144,1024]{0,1:T(8,128)(2,1)} %all-gather.9.cloned.1.call-done, f32[768,6144]{1,0:T(8,128)} %get-tuple-element.3, s32[6144]{0:T(1024)S(1)} %fusion.13, f32[768]{0:T(1024)S(1)} %log_add_fusion, s32[768]{0:T(1024)S(1)} %copy-done), kind=kOutput, calls=%fused_computation.4 | convolution fusion | flops 9691987968 | bytes 34633728 | tf_op jit(solution)/shard_map/dot_general | solution.py:38
  229.9 0.0 reduce-scatter.5.cloned.1.call-start
  229.9 58.3 %all-gather.11.cloned.1.call-done = bf16[6144,1024]{0,1:T(8,128)(2,1)} async-done(((bf16[384,1024]{0,1:T(8,128)(2,1)}), bf16[6144,1024]{0,1:T(8,128)(2,1)}) %all-gather.11.cloned.1.call-update) | async-done | bytes 12582928 | tf_op jit(solution)/shard_map/all_gather | solution.py:45
  288.2 35.9 %fusion.16 = f32[768,1024]{1,0:T(8,128)} fusion(bf16[6144,1024]{0,1:T(8,128)(2,1)} %all-gather.11.cloned.1.call-done, bf16[768,1024]{1,0:T(8,128)(2,1)} %all-gather.13.cloned.1.call-done, f32[768]{0:T(1024)S(1)} %add_convert_fusion, f32[6144]{0:T(1024)S(1)} %bitcast.30, f32[6144]{0:T(1024)S(1)} %bitcast.29), kind=kOutput, calls=%fused_computation.27 | convolution fusion | flops 19355664384 | bytes 17353728 | tf_op jit(solution)/shard_map/dot_general | solution.py:65
  324.2 7.8 %reduce-scatter.3.cloned.1.call-done = f32[768,512]{1,0:T(8,128)} async-done(((f32[768,1024]{1,0:T(8,128)}), f32[768,512]{1,0:T(8,128)}) %reduce-scatter.3.cloned.1.call-update) | async-done | bytes 1572880 | tf_op jit(solution)/shard_map/reduce_scatter | solution.py:39
  332.0 2.4 convert_element_type.30
  334.4 43.2 %reduce-scatter.5.cloned.1.call-done = f32[768,512]{1,0:T(8,128)} async-done(((f32[768,1024]{1,0:T(8,128)}), f32[768,512]{1,0:T(8,128)}) %reduce-scatter.5.cloned.1.call-update) | async-done | bytes 1572880 | tf_op jit(solution)/shard_map/reduce_scatter | solution.py:68
  377.5 2.4 convert_element_type.35
  (17 shorter events, 0.3 us)
Async XLA Ops:
  7.2 66.4 %all-gather.7.cloned.1.call-start = ((), (), s32[]{:S(2)}) async-start(), calls=%async_computation.4 | async-start | bytes 2359296 | tf_op jit(solution)/shard_map/all_gather | solution.py:15
  7.9 147.0 %all-gather.9.cloned.1.call-start = ((), (), s32[]{:S(2)}) async-start(), calls=%async_computation.5 | async-start | bytes 13369344 | tf_op jit(solution)/shard_map/all_gather | solution.py:16
  27.2 202.7 %all-gather.13.cloned.1.call-start = ((), (), s32[]{:S(2)}) async-start(), calls=%async_computation.8 | async-start | bytes 2359296 | tf_op jit(solution)/shard_map/all_gather | solution.py:43
  28.0 260.3 %all-gather.11.cloned.1.call-start = ((), (), s32[]{:S(2)}) async-start(), calls=%async_computation.7 | async-start | bytes 13369344 | tf_op jit(solution)/shard_map/all_gather | solution.py:45
  50.3 281.7 %reduce-scatter.3.cloned.1.call-start = ((), (), s32[]{:S(2)}) async-start(), calls=%async_computation.6 | async-start | bytes 4718592 | tf_op jit(solution)/shard_map/reduce_scatter | solution.py:39
  171.9 39.2 %copy-start = (s32[768]{0:T(1024)S(1)}, s32[768]{0:T(1024)}, u32[]{:S(2)}) copy-start(s32[768]{0:T(1024)} %param.5) | copy-start | bytes 9220
  229.9 147.6 %reduce-scatter.5.cloned.1.call-start = ((), (), s32[]{:S(2)}) async-start(), calls=%async_computation.9 | async-start | bytes 4718592 | tf_op jit(solution)/shard_map/reduce_scatter | solution.py:68
Sparse Core Ops, SparseCore 0:
  9.5 38.7 all-gather.6
  51.1 103.7 all-gather.8
  156.5 25.4 all-gather.12
  184.5 103.6 all-gather.10
  290.3 41.6 reduce-scatter.2
  334.1 43.3 reduce-scatter.4
where the time goes:
time: 387 us
  waiting for transfers between devices  192 us (50%)
  blocking collectives  91.1 us (24%)
  matrix products  71.6 us (19%)
  other arithmetic  15.1 us (4%)
  between operations  14.1 us (4%)
    all_gather x1, waiting for transfers between devices, local(): passage_block = lax.all_gather(relaid, 'dp', axis=0, tiled=True)  81.4 us
    all_gather x1, waiting for transfers between devices, local(): all_queries = lax.all_gather(query_relaid, 'dp', axis=0, tiled=True)  58.3 us
    reduce_scatter x1, waiting for transfers between devices, local(): lax.psum_scatter(own_terms, 'mp', scatter_dimension=1, tiled=True)  43.2 us
    dot_general x1, matrix products, local(): lax.dot_general(own_grad, all_queries, (((0,), (0,)), ((), ())), preferre...  35.9 us
    all_gather x1, blocking collectives, local(): lax.all_gather(own_targets, 'dp', axis=0, tiled=True)  22.4 us
    all_to_all x1, blocking collectives, local(): lax.all_to_all(queries, 'mp', split_axis=0, concat_axis=1, tiled=True)  21.1 us
    all_gather x1, blocking collectives, local(): lax.all_gather(own_log, 'dp', axis=0, tiled=True)  19.4 us
    dot_general x1, matrix products, local(): jnp.dot(softmax_grad, passage_block, preferred_element_type=jnp.float32)  18.8 us
  transfers between devices with their start and end apart: 6, of which 4 were waited for; matrix products, arithmetic and copies ran while one was open for 22% of the time, Pallas kernels for 0%

commit v1 on v0

--- a/solution.py
+++ b/solution.py
@@ -4,6 +4,18 @@
 import jax.numpy as jnp
 from jax import lax
 from jax.sharding import PartitionSpec as P
+
+
+def reduce_width(terms):
+    count = lax.axis_size("mp")
+    index = lax.axis_index("mp")
+    width = terms.shape[1] // count
+    total = lax.dynamic_slice_in_dim(terms, index * width, width, 1)
+    for hop in range(1, count):
+        sent = lax.dynamic_slice_in_dim(terms, (index + hop) % count * width, width, 1)
+        ring = [(d, (d + hop) % count) for d in range(count)]
+        total += lax.ppermute(sent.astype(jnp.bfloat16), "mp", ring).astype(jnp.float32)
+    return total.astype(jnp.bfloat16)
 
 
 def local(queries, passages, positive):
@@ -36,9 +48,7 @@
     onehot = (column_ids[None, :] == positive[:, None]).astype(jnp.float32)
     softmax_grad = (jnp.exp(scores - log_total[:, None]) - onehot).astype(jnp.bfloat16)
     query_terms = jnp.dot(softmax_grad, passage_block, preferred_element_type=jnp.float32)
-    grad_queries = lax.psum_scatter(query_terms, "mp", scatter_dimension=1, tiled=True).astype(
-        jnp.bfloat16
-    )
+    grad_queries = reduce_width(query_terms)
     group_index = lax.axis_index("dp")
     own_passages = lax.all_gather(passages, "mp", axis=1, tiled=True)
     query_relaid = lax.all_to_all(queries, "mp", split_axis=0, concat_axis=1, tiled=True)
@@ -65,9 +75,7 @@
     own_terms = lax.dot_general(
         own_grad, all_queries, (((0,), (0,)), ((), ())), preferred_element_type=jnp.float32
     )
-    grad_passages = lax.psum_scatter(own_terms, "mp", scatter_dimension=1, tiled=True).astype(
-        jnp.bfloat16
-    )
+    grad_passages = reduce_width(own_terms)
     return (grad_queries, grad_passages)
 
 

time: 387 us -> 356 us (0.920)
  waiting for transfers between devices: 192 us -> 155 us
    reduce_scatter x2 -> x0, waiting for transfers between devices: 51 us -> none  [the longest x1 43.2 us: local(): lax.psum_scatter(own_terms, 'mp', scatter_dimension=1, tiled=True)]
    ppermute x0 -> x2, waiting for transfers between devices: none -> 16.2 us  [reduce_width(): lax.ppermute(sent.astype(jnp.bfloat16), 'mp', ring).astype(jnp.float32)]
  transfers between devices with their start and end apart: 6 -> 6, of which waited for: 4 -> 3; matrix products, arithmetic and copies ran while one was open for 22% -> 25% of each run, Pallas kernels for 0% -> 0%
where the time goes in v1:
time: 356 us
  waiting for transfers between devices  155 us (44%)
  blocking collectives  90.9 us (26%)
  matrix products  71.1 us (20%)
  other arithmetic  15.5 us (4%)
  between operations  13.8 us (4%)
  local copies, waits for them, and re-layouts  5.8 us (2%)
    all_gather x1, waiting for transfers between devices, local(): passage_block = lax.all_gather(relaid, 'dp', axis=0, tiled=True)  81.4 us
    all_gather x1, waiting for transfers between devices, local(): all_queries = lax.all_gather(query_relaid, 'dp', axis=0, tiled=True)  56.3 us
    dot_general x1, matrix products, local(): lax.dot_general(own_grad, all_queries, (((0,), (0,)), ((), ())), preferre...  35.8 us
    all_gather x1, blocking collectives, local(): lax.all_gather(own_targets, 'dp', axis=0, tiled=True)  22.4 us
    all_to_all x1, blocking collectives, local(): lax.all_to_all(queries, 'mp', split_axis=0, concat_axis=1, tiled=True)  21.1 us
    all_gather x1, blocking collectives, local(): lax.all_gather(own_log, 'dp', axis=0, tiled=True)  19.2 us
    dot_general x1, matrix products, local(): jnp.dot(softmax_grad, passage_block, preferred_element_type=jnp.float32)  18.2 us
    all_to_all x1, blocking collectives, local(): lax.all_to_all(passages, 'mp', split_axis=0, concat_axis=1, tiled=True)  18.1 us
  transfers between devices with their start and end apart: 6, of which 3 were waited for; matrix products, arithmetic and copies ran while one was open for 25% of the time, Pallas kernels for 0%

profile of v1, /device:TPU:0, one launch (start us, length us, event | category | flops | bytes accessed | tf_op | source)
XLA Modules:
  0.0 355.7 jit_solution(3357718568908290276)
XLA Ops:
  7.2 0.7 all-gather.7.cloned.1.call-update
  7.9 18.1 %all_to_all.38 = bf16[2,384,512]{2,1,0:T(8,128)(2,1)S(1)} all-to-all(bf16[2,384,512]{2,1,0:T(8,128)(2,1)} %bitcast.24), channel_id=1, replica_groups=mesh['dp'=16,'mp'=2] {'mp'}, dimensions={0} | all-to-all | bytes 1572864 | tf_op jit(solution)/shard_map/all_to_all | solution.py:25
  26.0 1.2 copy.7
  27.3 0.7 all-gather.13.cloned.1.call-update
  28.0 21.1 %all_to_all.39 = bf16[2,384,512]{2,1,0:T(8,128)(2,1)S(1)} all-to-all(bf16[2,384,512]{2,1,0:T(8,128)(2,1)} %bitcast.23), channel_id=1, replica_groups=mesh['dp'=16,'mp'=2] {'mp'}, dimensions={0} | all-to-all | bytes 1572864 | tf_op jit(solution)/shard_map/all_to_all | solution.py:54
  49.1 1.2 copy.8
  50.3 0.8 dynamic-slice_convert_fusion.2
  51.0 22.4 %all-gather.1 = f32[16,1,384]{2,1,0:T(1,128)S(1)} all-gather(f32[1,1,384]{2,1,0:T(1,128)S(1)} %reshape.42), channel_id=1, replica_groups=mesh['dp'=16,'mp'=2] {'dp'}, dimensions={0}, use_global_device_ids=true | all-gather | bytes 26112 | tf_op jit(solution)/shard_map/all_gather | solution.py:62
  73.5 81.4 %all-gather.9.cloned.1.call-done = bf16[6144,1024]{0,1:T(8,128)(2,1)} async-done(((bf16[384,1024]{0,1:T(8,128)(2,1)}), bf16[6144,1024]{0,1:T(8,128)(2,1)}) %all-gather.9.cloned.1.call-update) | async-done | bytes 12582928 | tf_op jit(solution)/shard_map/all_gather | solution.py:28
  154.9 17.1 %multiply_reduce_fusion = (f32[768]{0:T(1024)S(1)}, f32[768,6144]{1,0:T(8,128)}) fusion(bf16[768,1024]{1,0:T(8,128)(2,1)} %all-gather.7.cloned.1.call-done, bf16[6144,1024]{0,1:T(8,128)(2,1)} %all-gather.9.cloned.1.call-done), kind=kOutput, calls=%fused_computation.3 | convolution fusion | flops 9673112576 | bytes 33033216 | tf_op jit(solution)/shard_map/dot_general | solution.py:32
  172.0 5.2 %pmax.7 = f32[768]{0:T(1024)S(1)} all-reduce(f32[768]{0:T(1024)S(1)} %get-tuple-element.2), channel_id=1, replica_groups=mesh['dp'=16,'mp'=2] {'mp'}, use_global_device_ids=true, to_apply=%region_1.0 | all-reduce | flops 768 | bytes 6144 | tf_op jit(solution)/shard_map/pmax | solution.py:41
  177.2 9.5 %exponential_reduce_fusion = f32[768]{0:T(1024)S(1)} fusion(f32[768,6144]{1,0:T(8,128)} %get-tuple-element.3, f32[768]{0:T(1024)S(1)} %pmax.7), kind=kLoop, calls=%fused_computation.2 | loop fusion | flops 14155008 | bytes 18880512 | tf_op jit(solution)/shard_map/reduce_sum | solution.py:42
  186.8 4.9 %psum.7 = f32[768]{0:T(1024)S(1)} all-reduce(f32[768]{0:T(1024)S(1)} %exponential_reduce_fusion), channel_id=1, replica_groups=mesh['dp'=16,'mp'=2] {'mp'}, use_global_device_ids=true, to_apply=%region_3.0 | all-reduce | flops 768 | bytes 6144 | tf_op jit(solution)/shard_map/psum | solution.py:42
  191.8 18.2 %fusion = f32[768,1024]{1,0:T(8,128)S(1)} fusion(bf16[6144,1024]{0,1:T(8,128)(2,1)} %all-gather.9.cloned.1.call-done, f32[768,6144]{1,0:T(8,128)} %get-tuple-element.3, s32[6144]{0:T(1024)S(1)} %fusion.13, f32[768]{0:T(1024)S(1)} %log_add_fusion, s32[768]{0:T(1024)S(1)} %copy-done), kind=kOutput, calls=%fused_computation.4 | convolution fusion | flops 9691987968 | bytes 34633728 | tf_op jit(solution)/shard_map/dot_general | solution.py:50
  210.0 1.0 dynamic-slice_convert_fusion.1
  211.0 1.6 collective-permute-start
  212.6 19.2 %all-gather = f32[16,1,384]{2,1,0:T(1,128)S(1)} all-gather(f32[1,1,384]{2,1,0:T(1,128)S(1)} %reshape.40), channel_id=1, replica_groups=mesh['dp'=16,'mp'=2] {'dp'}, dimensions={0}, use_global_device_ids=true | all-gather | bytes 26112 | tf_op jit(solution)/shard_map/all_gather | solution.py:61
  231.8 56.3 %all-gather.11.cloned.1.call-done = bf16[6144,1024]{0,1:T(8,128)(2,1)} async-done(((bf16[384,1024]{0,1:T(8,128)(2,1)}), bf16[6144,1024]{0,1:T(8,128)(2,1)}) %all-gather.11.cloned.1.call-update) | async-done | bytes 12582928 | tf_op jit(solution)/shard_map/all_gather | solution.py:55
  288.2 35.8 %fusion.16 = f32[768,1024]{1,0:T(8,128)} fusion(bf16[6144,1024]{0,1:T(8,128)(2,1)} %all-gather.11.cloned.1.call-done, bf16[768,1024]{1,0:T(8,128)(2,1)} %all-gather.13.cloned.1.call-done, f32[768]{0:T(1024)S(1)} %add_convert_fusion.2, f32[6144]{0:T(1024)S(1)} %bitcast.30, f32[6144]{0:T(1024)S(1)} %bitcast.29), kind=kOutput, calls=%fused_computation.31 | convolution fusion | flops 19355664384 | bytes 17353728 | tf_op jit(solution)/shard_map/dot_general | solution.py:75
  323.9 2.4 dynamic-slice_convert_fusion
  326.3 1.5 collective-permute-start.1
  327.8 2.3 add_convert_fusion.1
  330.2 16.2 %collective-permute-done.1 = bf16[768,512]{1,0:T(8,128)(2,1)} collective-permute-done((bf16[768,512]{1,0:T(8,128)(2,1)}, bf16[768,512]{1,0:T(8,128)(2,1)}, u32[]{:S(2)}, u32[]{:S(2)}) %collective-permute-start.1) | collective-permute-done | bytes 786464 | tf_op jit(solution)/shard_map/ppermute | solution.py:17
  346.3 2.8 add_convert_fusion
  (17 shorter events, 0.3 us)
Async XLA Ops:
  7.2 66.3 %all-gather.7.cloned.1.call-start = ((), (), s32[]{:S(2)}) async-start(), calls=%async_computation.2 | async-start | bytes 2359296 | tf_op jit(solution)/shard_map/all_gather | solution.py:27
  7.9 147.0 %all-gather.9.cloned.1.call-start = ((), (), s32[]{:S(2)}) async-start(), calls=%async_computation.3 | async-start | bytes 13369344 | tf_op jit(solution)/shard_map/all_gather | solution.py:28
  27.2 204.6 %all-gather.13.cloned.1.call-start = ((), (), s32[]{:S(2)}) async-start(), calls=%async_computation.5 | async-start | bytes 2359296 | tf_op jit(solution)/shard_map/all_gather | solution.py:53
  27.9 260.2 %all-gather.11.cloned.1.call-start = ((), (), s32[]{:S(2)}) async-start(), calls=%async_computation.4 | async-start | bytes 13369344 | tf_op jit(solution)/shard_map/all_gather | solution.py:55
  172.0 19.8 %copy-start = (s32[768]{0:T(1024)S(1)}, s32[768]{0:T(1024)}, u32[]{:S(2)}) copy-start(s32[768]{0:T(1024)} %param.5) | copy-start | bytes 9220
  211.0 116.8 %collective-permute-start = (bf16[768,512]{1,0:T(8,128)(2,1)}, bf16[768,512]{1,0:T(8,128)(2,1)}, u32[]{:S(2)}, u32[]{:S(2)}) collective-permute-start(bf16[768,512]{1,0:T(8,128)(2,1)} %dynamic-slice_convert_fusion.1), channel_id=1, source_target_pairs={{0,1},{1,0},{2,3},{3,2},{4,5},{5,4},{6,7},{7,6},{8,9},{9,8},{10,11... | collective-permute-start | bytes 2359304 | tf_op jit(solution)/shard_map/ppermute | solution.py:17
  326.3 20.0 %collective-permute-start.1 = (bf16[768,512]{1,0:T(8,128)(2,1)}, bf16[768,512]{1,0:T(8,128)(2,1)}, u32[]{:S(2)}, u32[]{:S(2)}) collective-permute-start(bf16[768,512]{1,0:T(8,128)(2,1)} %dynamic-slice_convert_fusion), channel_id=1, source_target_pairs={{0,1},{1,0},{2,3},{3,2},{4,5},{5,4},{6,7},{7,6},{8,9},{9,8},{10,11... | collective-permute-start | bytes 2359304 | tf_op jit(solution)/shard_map/ppermute | solution.py:17
Sparse Core Ops, SparseCore 0:
  9.5 38.7 all-gather.6
  51.1 103.7 all-gather.8
  156.5 25.4 all-gather.12
  184.5 103.5 all-gather.10
